TPU v7x, 32 devices: a whole 2x2x4 slice. The times are simulated.
32 devices in a mesh: gx: 8 (over z, y), gy: 4 (over x, core).
Axes of the slice: x: 2, y: 2, z: 4, core: 2. Of those that a mesh axis runs over, the one named last changes fastest.
Arguments:
- goal_embed: bfloat16 [4096, 128], P(('gx', 'gy')), may hold values from -6 to 6
- goal_bins: int32 [4096], P(('gx', 'gy')), may hold values from 0 to 2047, as said below
- goal_weights: float32 [4096], P(('gx', 'gy')), may hold values from 0.1 to 10
Outputs:
- bin_mean: float32 [2048, 128], P(('gx', 'gy'))
- rarity: float32 [2048], P(('gx', 'gy'))
Inputs may be any that keep to these rules, and one draw needn't show every extreme that they name: `goal_bins`: bin b belongs to owner b // 64, owners numbered in the order of gx then gy. Of the goals of one device, at most 8 fall in the bins of one owner; some owner receives exactly 8 goals from every device.
All inputs are finite; a program needn't handle non-finite values.
Results may differ from a plain program's by a relative error of at most 0.0029.
Values may be sent and summed in bfloat16 or wider, within the bound.
A program may use at most 64 MiB of HBM per device.

v0:
```python
import functools

import jax
import jax.numpy as jnp
from jax import lax
from jax.experimental import pallas as pl
from jax.experimental.pallas import tpu as pltpu
from jax.sharding import PartitionSpec as P

BINS_DEV = 64
MESH = pl.DeviceIdType.MESH


def each(count, body):
    if count <= 64:
        for k in range(count):
            body(k)
    else:
        lax.fori_loop(0, count, lambda k, c: (body(k), c)[1], 0)


def split3(x):
    hi = x.astype(jnp.bfloat16).astype(jnp.float32)
    rest = x - hi
    mid = rest.astype(jnp.bfloat16).astype(jnp.float32)
    return hi, mid, rest - mid


def kernel(across, along, stride, embed_hbm, bins_hbm, weights_hbm, mean_ref, rarity_ref, send, recv, send_sem, recv_sem, embed_ref, bins_ref, weights_ref, in_sem):
    loads = [pltpu.make_async_copy(a, b, in_sem.at[i]) for i, (a, b) in enumerate(((bins_hbm, bins_ref), (weights_hbm, weights_ref), (embed_hbm, embed_ref)))]
    for c in loads:
        c.start()
    n = across * along
    goals, width = embed_ref.shape
    me = lax.axis_index("gx") * along + lax.axis_index("gy")

    def device(k):
        d = lax.rem(me + k + 1, n)
        return {"gx": d // along, "gy": lax.rem(d, along)}

    barrier = pltpu.get_barrier_semaphore()
    each(n - 1, lambda k: pl.semaphore_signal(barrier, inc=1, device_id=device(k), device_id_type=MESH))

    for c in loads:
        c.wait()
    bins_row = jnp.broadcast_to(bins_ref[...], (goals, goals))
    weights_row = jnp.broadcast_to(weights_ref[...], (goals, goals))
    bins_col = bins_row.T
    weights_col = weights_row.T
    shift = BINS_DEV.bit_length() - 1
    owners_row = lax.shift_right_logical(bins_row, shift)
    owners_col = lax.shift_right_logical(bins_col, shift)
    sub = lax.broadcasted_iota(jnp.int32, (goals, goals), 0)
    lane = lax.broadcasted_iota(jnp.int32, (goals, goals), 1)
    earlier = (owners_row == owners_col) & (sub < lane)
    place = jnp.sum(earlier.astype(jnp.float32), axis=0, keepdims=True).astype(jnp.int32)
    ahead = owners_row[:1] - me - 1
    ahead = jnp.where(ahead < 0, ahead + n, ahead)
    rows_iota = lax.broadcasted_iota(jnp.int32, (n * stride, goals), 0)
    base = ahead * stride
    pick = (rows_iota == base + place).astype(jnp.bfloat16)
    group = ((rows_iota >= base) & (rows_iota < base + stride)).astype(jnp.bfloat16)

    offset = bins_col - owners_col * BINS_DEV
    place_col = jnp.sum(((owners_row == owners_col) & (lane < sub)).astype(jnp.float32), axis=1, keepdims=True)
    hit = (lane == offset) | (lane == offset + BINS_DEV)
    masses = jnp.zeros((n * stride, goals), jnp.float32)
    for part in split3(weights_col):
        spread = jnp.where(hit, part, 0.0).astype(jnp.bfloat16)
        masses = masses + jnp.dot(group, spread, preferred_element_type=jnp.float32)
    spot = jnp.where(lane == place_col.astype(jnp.int32) + BINS_DEV, offset.astype(jnp.float32), 0.0)
    offsets = jnp.dot(group, spot.astype(jnp.bfloat16), preferred_element_type=jnp.float32)
    local = jnp.sum(weights_ref[...], axis=1, keepdims=True)
    t_lane = lax.broadcasted_iota(jnp.int32, (1, goals), 1)
    extra = jnp.zeros((1, goals), jnp.float32)
    for i, part in enumerate(split3(local)):
        extra = jnp.where(t_lane == BINS_DEV + stride + i, part, extra)
    hi, mid, lo = split3(masses)
    low_half = lax.broadcasted_iota(jnp.int32, (n * stride, goals), 1) < BINS_DEV
    line = lax.rem(rows_iota, stride)
    marks = jnp.where(line == 0, jnp.where(low_half, lo, offsets + extra), jnp.where(low_half, hi, mid))
    scaled = (weights_col[:, :width] * embed_ref[...].astype(jnp.float32)).astype(jnp.bfloat16)
    rows = jnp.dot(pick, scaled, preferred_element_type=jnp.float32)
    full = jnp.concatenate([rows.reshape(n, stride, width), marks.reshape(n, stride, goals)], axis=1)
    full = full.astype(jnp.bfloat16)
    send[...] = full[: n - 1]
    recv[n - 1] = full[n - 1]

    pl.semaphore_wait(barrier, n - 1)

    def start(k):
        pltpu.make_async_remote_copy(
            src_ref=send.at[k, pl.ds(0, stride + 2)],
            dst_ref=recv.at[k, pl.ds(0, stride + 2)],
            send_sem=send_sem,
            recv_sem=recv_sem,
            device_id=device(k),
            device_id_type=MESH,
        ).start()

    each(n - 1, start)
    landed = recv.at[pl.ds(0, n - 1), pl.ds(0, stride + 2)]
    pltpu.make_async_copy(landed, landed, recv_sem).wait()

    data = recv[...].astype(jnp.float32)
    tags = data[:, stride:]
    s_sub = lax.broadcasted_iota(jnp.int32, (n, stride, goals), 1)
    s_lane = lax.broadcasted_iota(jnp.int32, (n, stride, goals), 2)
    spread = jnp.where(s_lane == s_sub + BINS_DEV, jnp.broadcast_to(tags[:, :1], (n, stride, goals)), 0.0)
    labels = jnp.sum(spread, axis=2, keepdims=True).astype(jnp.int32)
    choose = (s_lane == labels).astype(jnp.float32).reshape(n * stride, goals).astype(jnp.bfloat16)
    values = data[:, :stride].reshape(n * stride, width).astype(jnp.bfloat16)
    sums = lax.dot_general(choose, values, (((0,), (0,)), ((), ())), preferred_element_type=jnp.float32)
    added = jnp.sum(tags, axis=0)
    low, high = added[:1], added[1:2]
    mass = high + pltpu.roll(high, goals - BINS_DEV, 1) + low
    total = jnp.sum(
        jnp.where((t_lane >= BINS_DEV + stride) & (t_lane < BINS_DEV + stride + 3), low, 0.0), axis=1, keepdims=True
    )
    mass_col = jnp.broadcast_to(mass, (goals, goals)).T
    mean_ref[...] = sums[:BINS_DEV] / (mass_col[:BINS_DEV, :width] + 1.0)
    rarity_ref[...] = jnp.log(total / (BINS_DEV * n)) - jnp.log(mass[:, :BINS_DEV] + 1.0)
    sent = send.at[:, pl.ds(0, stride + 2)]
    pltpu.make_async_copy(sent, sent, send_sem).wait()


def put(mean, rarity, mean_hbm, rarity_hbm, sem):
    copies = [pltpu.make_async_copy(mean, mean_hbm, sem.at[0]), pltpu.make_async_copy(rarity, rarity_hbm, sem.at[1])]
    for c in copies:
        c.start()
    for c in copies:
        c.wait()


def shards(goal_embed, goal_bins, goal_weights):
    goals, width = goal_embed.shape
    across = lax.axis_size("gx")
    along = lax.axis_size("gy")
    n = across * along
    capacity = max(2, 2 * goals // n)
    stride = -(-capacity // 8) * 8
    mean, rarity = pl.pallas_call(
        functools.partial(kernel, across, along, stride),
        out_shape=(
            pltpu.VMEM((BINS_DEV, width), jnp.float32),
            pltpu.VMEM((1, BINS_DEV), jnp.float32),
        ),
        in_specs=[pl.BlockSpec(memory_space=pl.ANY)] * 3,
        out_specs=(pl.BlockSpec(memory_space=pltpu.VMEM),) * 2,
        scratch_shapes=[
            pltpu.VMEM((n - 1, 2 * stride, width), jnp.bfloat16),
            pltpu.VMEM((n, 2 * stride, width), jnp.bfloat16),
            pltpu.SemaphoreType.DMA,
            pltpu.SemaphoreType.DMA,
            pltpu.VMEM((goals, width), jnp.bfloat16),
            pltpu.VMEM((1, goals), jnp.int32),
            pltpu.VMEM((1, goals), jnp.float32),
            pltpu.SemaphoreType.DMA((3,)),
        ],
        compiler_params=pltpu.CompilerParams(collective_id=0, has_side_effects=True),
    )(goal_embed, goal_bins.reshape(1, goals), goal_weights.reshape(1, goals))
    mean, rarity = pl.pallas_call(
        put,
        out_shape=(
            jax.ShapeDtypeStruct((BINS_DEV, width), jnp.float32),
            jax.ShapeDtypeStruct((1, BINS_DEV), jnp.float32),
        ),
        in_specs=[pl.BlockSpec(memory_space=pltpu.VMEM)] * 2,
        out_specs=(pl.BlockSpec(memory_space=pl.ANY),) * 2,
        scratch_shapes=[pltpu.SemaphoreType.DMA((2,))],
    )(pltpu.with_memory_space_constraint(mean, pltpu.VMEM), pltpu.with_memory_space_constraint(rarity, pltpu.VMEM))
    return mean, rarity.reshape(BINS_DEV)


def solution(mesh):
    in_specs = (P(("gx", "gy"), None), P(("gx", "gy")), P(("gx", "gy")))
    out_specs = (P(("gx", "gy"), None), P(("gx", "gy")))
    return jax.shard_map(shards, mesh=mesh, in_specs=in_specs, out_specs=out_specs, check_vma=False)
```

profile of v0, /device:TPU:0, one launch (start us, length us, event | category | flops | bytes accessed | tf_op | source)
XLA Modules:
  0.0 11.3 jit_solution(14408205068196347873)
XLA Ops:
  0.6 10.0 %shard_map.50 = (f32[64,128]{1,0:T(8,128)S(1)}, f32[1,64]{1,0:T(1,128)S(1)}) custom-call(bf16[128,128]{1,0:T(8,128)(2,1)} %embed_hbm.1, s32[1,128]{1,0:T(1,128)} %bitcast.3, f32[1,128]{1,0:T(1,128)} %bitcast.4), custom_call_target="tpu_custom_call" | custom-call | tf_op jit(solution)/shard_map/pallas_call | solution.py:142
  10.7 0.6 %shard_map.51 = (f32[64,128]{1,0:T(8,128)}, f32[1,64]{1,0:T(1,128)}) custom-call(f32[64,128]{1,0:T(8,128)S(1)} %get-tuple-element.6.mean, f32[1,64]{1,0:T(1,128)S(1)} %get-tuple-element.7.rarity), custom_call_target="tpu_custom_call" | custom-call | tf_op jit(solution)/shard_map/pallas_call | solution.py:162
where the time goes:
time: 11.5 us; the launch traced here: 11.3 us
  Pallas kernels  10.7 us (93%)
  between operations  0.64 us (6%)
    pallas_call x1, Pallas kernels, shards(): pl.pallas_call(functools.partial(kernel, across, along, stride), out_shap...  10 us
    pallas_call x1, Pallas kernels, shards(): pl.pallas_call(put, out_shape=(jax.ShapeDtypeStruct((BINS_DEV, width), jn...  0.64 us

commit v1 on v0

v1 whole, which is shorter than its diff:
```python
import functools

import jax
import jax.numpy as jnp
from jax import lax
from jax.experimental import pallas as pl
from jax.experimental.pallas import tpu as pltpu
from jax.sharding import PartitionSpec as P

BINS_DEV = 64
MARKS = 4
LATE = 4
LOGICAL = pl.DeviceIdType.LOGICAL


def each(first, last, body):
    if last - first <= 64:
        for k in range(first, last):
            body(k)
    else:
        lax.fori_loop(first, last, lambda k, c: (body(k), c)[1], 0)


def split3(x):
    hi = x.astype(jnp.bfloat16).astype(jnp.float32)
    rest = x - hi
    mid = rest.astype(jnp.bfloat16).astype(jnp.float32)
    return hi, mid, rest - mid


def split2(x):
    hi = x.astype(jnp.bfloat16).astype(jnp.float32)
    return hi, x - hi


def kernel(across, along, stride, embed_hbm, bins_hbm, weights_hbm, mean_ref, rarity_ref, send, recv, send_sem, recv_sem, gate, embed_ref, bins_ref, weights_ref, in_sem):
    loads = [pltpu.make_async_copy(a, b, in_sem.at[i]) for i, (a, b) in enumerate(((bins_hbm, bins_ref), (weights_hbm, weights_ref), (embed_hbm, embed_ref)))]
    for c in loads:
        c.start()
    n = across * along
    goals, width = embed_ref.shape
    sent_rows = stride + MARKS
    me = lax.axis_index("gx") * along + lax.axis_index("gy")

    late = min(LATE, n // 2)
    early = n - late
    is_late = me >= early

    def signal(sem, d):
        pl.semaphore_signal(sem, inc=1, device_id=d, device_id_type=LOGICAL)

    barrier = pltpu.get_barrier_semaphore()
    each(0, n, lambda d: pl.when((me != d) & (me < early))(lambda: signal(barrier, d)))

    loads[0].wait()
    loads[1].wait()
    bins = bins_ref[...]
    weights = weights_ref[...]
    shift = BINS_DEV.bit_length() - 1
    owners = lax.shift_right_logical(bins, shift)
    labels = (bins - owners * BINS_DEV).astype(jnp.float32)
    owners_col = jnp.broadcast_to(owners, (goals, goals)).T
    weights_col = jnp.broadcast_to(weights, (goals, goals)).T
    sub = lax.broadcasted_iota(jnp.int32, (goals, goals), 0)
    lane = lax.broadcasted_iota(jnp.int32, (goals, goals), 1)
    earlier = (owners_col == owners) & (sub < lane)
    place = jnp.sum(earlier.astype(jnp.float32), axis=0, keepdims=True).astype(jnp.int32)
    loads[2].wait()
    rows_iota = lax.broadcasted_iota(jnp.int32, (n * stride, goals), 0)
    pick = (rows_iota == owners * stride + place).astype(jnp.bfloat16)
    group = lax.shift_right_logical(rows_iota, stride.bit_length() - 1) == owners
    hi, lo = split2(weights)
    t_sub = lax.broadcasted_iota(jnp.int32, (stride, goals), 0)
    t_lane = lax.broadcasted_iota(jnp.int32, (stride, goals), 1)
    kinds = jnp.where(t_sub == 0, labels, jnp.where(t_sub == 1, hi, jnp.where(t_sub == 2, lo, 0.0)))
    kinds = jnp.broadcast_to(kinds[None], (n, stride, goals)).reshape(n * stride, goals)
    tagged = jnp.where(group, kinds, 0.0).astype(jnp.bfloat16)
    base = lax.rem(me, goals // stride) * stride
    spot = (sub == place + base).astype(jnp.bfloat16)
    marks = lax.dot_general(tagged, spot, (((1,), (1,)), ((), ())), preferred_element_type=jnp.float32)
    local = jnp.sum(weights, axis=1, keepdims=True)
    total = jnp.zeros((stride, goals), jnp.float32)
    for i, part in enumerate(split3(local)):
        total = jnp.where((t_sub == 3) & (t_lane == i), part, total)
    marks = marks.reshape(n, stride, goals) + total[None]
    scaled = (weights_col[:, :width] * embed_ref[...].astype(jnp.float32)).astype(jnp.bfloat16)
    rows = jnp.dot(pick, scaled, preferred_element_type=jnp.float32)
    send[...] = jnp.concatenate([rows.reshape(n, stride, width), marks], axis=1).astype(jnp.bfloat16)

    def start(d):
        pltpu.make_async_remote_copy(
            src_ref=send.at[d, pl.ds(0, sent_rows)],
            dst_ref=recv.at[me, pl.ds(0, sent_rows)],
            send_sem=send_sem,
            recv_sem=recv_sem,
            device_id=d,
            device_id_type=LOGICAL,
        ).start()

    pl.semaphore_wait(barrier, jnp.where(is_late, early, early - 1))
    pl.when(is_late)(lambda: each(0, early, lambda d: signal(gate, d)))
    each(0, early, lambda d: pl.when(me != d)(lambda: start(d)))
    pl.semaphore_wait(gate, jnp.where(is_late, 1, late))
    each(early, n, lambda d: pl.when(me == d - late)(lambda: signal(gate, d)))
    each(early, n, lambda d: pl.when(me != d)(lambda: start(d)))
    recv[me] = send[me]
    landed = recv.at[pl.ds(0, n - 1), pl.ds(0, sent_rows)]
    pltpu.make_async_copy(landed, landed, recv_sem).wait()

    data = recv[...].astype(jnp.float32)
    values = data[:, :stride].reshape(n * stride, width).astype(jnp.bfloat16)
    tags = data[:, stride:]
    per = goals // stride
    r_sub = lax.broadcasted_iota(jnp.int32, (BINS_DEV, goals), 0)
    r_lane = lax.broadcasted_iota(jnp.int32, (BINS_DEV, goals), 1)
    mass = jnp.zeros((BINS_DEV, goals), jnp.float32)
    chosen = []
    total = jnp.zeros((1, goals), jnp.float32)
    for q in range(0, n, per):
        added = jnp.sum(tags[q : q + per], axis=0)
        hit = r_sub == added[0:1].astype(jnp.int32)
        chosen.append(jnp.where(hit, 1.0, 0.0).astype(jnp.bfloat16))
        mass = mass + jnp.where(hit, added[1:2] + added[2:3], 0.0)
        total = total + added[3:4]
    choose = jnp.concatenate(chosen, axis=1)[:, : n * stride]
    sums = jnp.dot(choose, values, preferred_element_type=jnp.float32)
    mass_col = jnp.sum(mass, axis=1, keepdims=True) + 1.0
    total = jnp.sum(total, axis=1, keepdims=True)
    mean_ref[...] = sums * (1.0 / mass_col)
    mass_row = jnp.sum(jnp.where(r_sub == r_lane, mass_col, 0.0), axis=0, keepdims=True)
    rarity_ref[...] = (jnp.log(total / (BINS_DEV * n)) - jnp.log(mass_row))[:, :BINS_DEV]
    sent = send.at[pl.ds(0, n - 1), pl.ds(0, sent_rows)]
    pltpu.make_async_copy(sent, sent, send_sem).wait()


def put(mean, rarity, mean_hbm, rarity_hbm, sem):
    copies = [pltpu.make_async_copy(mean, mean_hbm, sem.at[0]), pltpu.make_async_copy(rarity, rarity_hbm, sem.at[1])]
    for c in copies:
        c.start()
    for c in copies:
        c.wait()


def shards(goal_embed, goal_bins, goal_weights):
    goals, width = goal_embed.shape
    across = lax.axis_size("gx")
    along = lax.axis_size("gy")
    n = across * along
    capacity = max(2, 2 * goals // n)
    stride = -(-capacity // 8) * 8
    mean, rarity = pl.pallas_call(
        functools.partial(kernel, across, along, stride),
        out_shape=(
            pltpu.VMEM((BINS_DEV, width), jnp.float32),
            pltpu.VMEM((1, BINS_DEV), jnp.float32),
        ),
        in_specs=[pl.BlockSpec(memory_space=pl.ANY)] * 3,
        out_specs=(pl.BlockSpec(memory_space=pltpu.VMEM),) * 2,
        scratch_shapes=[
            pltpu.VMEM((n, 2 * stride, width), jnp.bfloat16),
            pltpu.VMEM((n, 2 * stride, width), jnp.bfloat16),
            pltpu.SemaphoreType.DMA,
            pltpu.SemaphoreType.DMA,
            pltpu.SemaphoreType.REGULAR,
            pltpu.VMEM((goals, width), jnp.bfloat16),
            pltpu.VMEM((1, goals), jnp.int32),
            pltpu.VMEM((1, goals), jnp.float32),
            pltpu.SemaphoreType.DMA((3,)),
        ],
        compiler_params=pltpu.CompilerParams(collective_id=0, has_side_effects=True),
    )(goal_embed, goal_bins.reshape(1, goals), goal_weights.reshape(1, goals))
    mean, rarity = pl.pallas_call(
        put,
        out_shape=(
            jax.ShapeDtypeStruct((BINS_DEV, width), jnp.float32),
            jax.ShapeDtypeStruct((1, BINS_DEV), jnp.float32),
        ),
        in_specs=[pl.BlockSpec(memory_space=pltpu.VMEM)] * 2,
        out_specs=(pl.BlockSpec(memory_space=pl.ANY),) * 2,
        scratch_shapes=[pltpu.SemaphoreType.DMA((2,))],
    )(pltpu.with_memory_space_constraint(mean, pltpu.VMEM), pltpu.with_memory_space_constraint(rarity, pltpu.VMEM))
    return mean, rarity.reshape(BINS_DEV)


def solution(mesh):
    in_specs = (P(("gx", "gy"), None), P(("gx", "gy")), P(("gx", "gy")))
    out_specs = (P(("gx", "gy"), None), P(("gx", "gy")))
    return jax.shard_map(shards, mesh=mesh, in_specs=in_specs, out_specs=out_specs, check_vma=False)
```

time: 11.5 us -> 11.2 us (0.974)
  Pallas kernels: 10.7 us -> 10.4 us
    pallas_call x1, Pallas kernels: 10 us -> 9.74 us  [shards(): pl.pallas_call(functools.partial(kernel, across, along, stride), out_shap...]
where the time goes in v1:
time: 11.2 us; the launch traced here: 11 us
  Pallas kernels  10.4 us (93%)
  between operations  0.64 us (6%)
    pallas_call x1, Pallas kernels, shards(): pl.pallas_call(functools.partial(kernel, across, along, stride), out_shap...  9.74 us
    pallas_call x1, Pallas kernels, shards(): pl.pallas_call(put, out_shape=(jax.ShapeDtypeStruct((BINS_DEV, width), jn...  0.64 us

profile of v1, /device:TPU:0, one launch (start us, length us, event | category | flops | bytes accessed | tf_op | source)
XLA Modules:
  0.0 11.0 jit_solution(6208098949062680343)
XLA Ops:
  0.6 9.7 %shard_map.50 = (f32[64,128]{1,0:T(8,128)S(1)}, f32[1,64]{1,0:T(1,128)S(1)}) custom-call(bf16[128,128]{1,0:T(8,128)(2,1)} %embed_hbm.1, s32[1,128]{1,0:T(1,128)} %bitcast.3, f32[1,128]{1,0:T(1,128)} %bitcast.4), custom_call_target="tpu_custom_call" | custom-call | tf_op jit(solution)/shard_map/pallas_call | solution.py:151
  10.4 0.6 %shard_map.51 = (f32[64,128]{1,0:T(8,128)}, f32[1,64]{1,0:T(1,128)}) custom-call(f32[64,128]{1,0:T(8,128)S(1)} %get-tuple-element.6.mean, f32[1,64]{1,0:T(1,128)S(1)} %get-tuple-element.7.rarity), custom_call_target="tpu_custom_call" | custom-call | tf_op jit(solution)/shard_map/pallas_call | solution.py:172

commit v2 on v1

--- a/solution.py
+++ b/solution.py
@@ -9,7 +9,7 @@
 
 BINS_DEV = 64
 MARKS = 4
-LATE = 4
+LATE = 6
 LOGICAL = pl.DeviceIdType.LOGICAL
 
 
@@ -21,27 +21,32 @@
         lax.fori_loop(first, last, lambda k, c: (body(k), c)[1], 0)
 
 
-def split3(x):
-    hi = x.astype(jnp.bfloat16).astype(jnp.float32)
-    rest = x - hi
-    mid = rest.astype(jnp.bfloat16).astype(jnp.float32)
-    return hi, mid, rest - mid
-
-
 def split2(x):
     hi = x.astype(jnp.bfloat16).astype(jnp.float32)
     return hi, x - hi
 
 
-def kernel(across, along, stride, embed_hbm, bins_hbm, weights_hbm, mean_ref, rarity_ref, send, recv, send_sem, recv_sem, gate, embed_ref, bins_ref, weights_ref, in_sem):
-    loads = [pltpu.make_async_copy(a, b, in_sem.at[i]) for i, (a, b) in enumerate(((bins_hbm, bins_ref), (weights_hbm, weights_ref), (embed_hbm, embed_ref)))]
-    for c in loads:
-        c.start()
+def split3(x):
+    hi, rest = split2(x)
+    mid, low = split2(rest)
+    return hi, mid, low
+
+
+def tree(parts):
+    while len(parts) > 1:
+        parts = [sum(parts[i : i + 2]) for i in range(0, len(parts), 2)]
+    return parts[0]
+
+
+def kernel(across, along, stride, embed_hbm, bins_hbm, weights_hbm, mean_ref, rarity_ref, send, recv, send_sem, recv_sem, gate, embed_ref, pair_ref, in_sem, bins_ref, weights_ref):
+    pltpu.make_async_copy(bins_hbm, bins_ref, in_sem).start()
+    pltpu.make_async_copy(weights_hbm, weights_ref, in_sem).start()
+    embed_load = pltpu.make_async_copy(embed_hbm, embed_ref, send_sem)
+    embed_load.start()
     n = across * along
     goals, width = embed_ref.shape
     sent_rows = stride + MARKS
     me = lax.axis_index("gx") * along + lax.axis_index("gy")
-
     late = min(LATE, n // 2)
     early = n - late
     is_late = me >= early
@@ -52,39 +57,43 @@
     barrier = pltpu.get_barrier_semaphore()
     each(0, n, lambda d: pl.when((me != d) & (me < early))(lambda: signal(barrier, d)))
 
-    loads[0].wait()
-    loads[1].wait()
+    shift = BINS_DEV.bit_length() - 1
+    sub = lax.broadcasted_iota(jnp.int32, (goals, goals), 0)
+    lane = lax.broadcasted_iota(jnp.int32, (goals, goals), 1)
+    rows_iota = lax.broadcasted_iota(jnp.int32, (n * stride, goals), 0)
+    t_sub = lax.broadcasted_iota(jnp.int32, (stride, goals), 0)
+    t_lane = lax.broadcasted_iota(jnp.int32, (stride, goals), 1)
+    before = (sub < lane).astype(jnp.bfloat16)
+    pltpu.make_async_copy(pair_ref, pair_ref, in_sem).wait()
     bins = bins_ref[...]
     weights = weights_ref[...]
-    shift = BINS_DEV.bit_length() - 1
     owners = lax.shift_right_logical(bins, shift)
     labels = (bins - owners * BINS_DEV).astype(jnp.float32)
-    owners_col = jnp.broadcast_to(owners, (goals, goals)).T
+    hi, lo = split2(weights)
+    owners_row = jnp.broadcast_to(owners.astype(jnp.float32), (goals, goals)).astype(jnp.bfloat16)
+    same = jnp.where(owners_row.T == owners_row, before, jnp.bfloat16(0))
+    same = tree([same[i : i + 16] for i in range(0, goals, 16)])
+    place = jnp.sum(same.astype(jnp.float32), axis=0, keepdims=True).astype(jnp.int32)
     weights_col = jnp.broadcast_to(weights, (goals, goals)).T
-    sub = lax.broadcasted_iota(jnp.int32, (goals, goals), 0)
-    lane = lax.broadcasted_iota(jnp.int32, (goals, goals), 1)
-    earlier = (owners_col == owners) & (sub < lane)
-    place = jnp.sum(earlier.astype(jnp.float32), axis=0, keepdims=True).astype(jnp.int32)
-    loads[2].wait()
-    rows_iota = lax.broadcasted_iota(jnp.int32, (n * stride, goals), 0)
-    pick = (rows_iota == owners * stride + place).astype(jnp.bfloat16)
-    group = lax.shift_right_logical(rows_iota, stride.bit_length() - 1) == owners
-    hi, lo = split2(weights)
-    t_sub = lax.broadcasted_iota(jnp.int32, (stride, goals), 0)
-    t_lane = lax.broadcasted_iota(jnp.int32, (stride, goals), 1)
-    kinds = jnp.where(t_sub == 0, labels, jnp.where(t_sub == 1, hi, jnp.where(t_sub == 2, lo, 0.0)))
-    kinds = jnp.broadcast_to(kinds[None], (n, stride, goals)).reshape(n * stride, goals)
-    tagged = jnp.where(group, kinds, 0.0).astype(jnp.bfloat16)
+    embed_load.wait()
     base = lax.rem(me, goals // stride) * stride
     spot = (sub == place + base).astype(jnp.bfloat16)
+    kind = lax.rem(t_sub, MARKS)
+    kinds = jnp.where(kind == 0, labels, jnp.where(kind == 1, hi, jnp.where(kind == 2, lo, 0.0)))
+    half = n // 2
+    owner_of = jnp.where(t_sub < MARKS, 0, half)
+    tagged = jnp.concatenate([jnp.where(owner_of + o == owners, kinds, 0.0) for o in range(half)], axis=0).astype(jnp.bfloat16)
     marks = lax.dot_general(tagged, spot, (((1,), (1,)), ((), ())), preferred_element_type=jnp.float32)
+    marks = marks.reshape(half, stride, goals)
+    marks = jnp.concatenate([marks, jnp.roll(marks, -MARKS, axis=1)], axis=0)
+    scaled = (weights_col[:, :width] * embed_ref[...].astype(jnp.float32)).astype(jnp.bfloat16)
+    pick = (rows_iota == owners * stride + place).astype(jnp.bfloat16)
+    rows = jnp.dot(pick, scaled, preferred_element_type=jnp.float32)
     local = jnp.sum(weights, axis=1, keepdims=True)
     total = jnp.zeros((stride, goals), jnp.float32)
     for i, part in enumerate(split3(local)):
         total = jnp.where((t_sub == 3) & (t_lane == i), part, total)
-    marks = marks.reshape(n, stride, goals) + total[None]
-    scaled = (weights_col[:, :width] * embed_ref[...].astype(jnp.float32)).astype(jnp.bfloat16)
-    rows = jnp.dot(pick, scaled, preferred_element_type=jnp.float32)
+    marks = marks + total[None]
     send[...] = jnp.concatenate([rows.reshape(n, stride, width), marks], axis=1).astype(jnp.bfloat16)
 
     def start(d):
@@ -98,8 +107,8 @@
         ).start()
 
     pl.semaphore_wait(barrier, jnp.where(is_late, early, early - 1))
+    each(0, early, lambda d: pl.when(me != d)(lambda: start(d)))
     pl.when(is_late)(lambda: each(0, early, lambda d: signal(gate, d)))
-    each(0, early, lambda d: pl.when(me != d)(lambda: start(d)))
     pl.semaphore_wait(gate, jnp.where(is_late, 1, late))
     each(early, n, lambda d: pl.when(me == d - late)(lambda: signal(gate, d)))
     each(early, n, lambda d: pl.when(me != d)(lambda: start(d)))
@@ -113,19 +122,18 @@
     per = goals // stride
     r_sub = lax.broadcasted_iota(jnp.int32, (BINS_DEV, goals), 0)
     r_lane = lax.broadcasted_iota(jnp.int32, (BINS_DEV, goals), 1)
-    mass = jnp.zeros((BINS_DEV, goals), jnp.float32)
-    chosen = []
-    total = jnp.zeros((1, goals), jnp.float32)
+    bin_of = r_sub.astype(jnp.float32)
+    masses, chosen, totals = [], [], []
     for q in range(0, n, per):
-        added = jnp.sum(tags[q : q + per], axis=0)
-        hit = r_sub == added[0:1].astype(jnp.int32)
+        added = tree([tags[s] for s in range(q, min(q + per, n))])
+        hit = bin_of == added[0:1]
         chosen.append(jnp.where(hit, 1.0, 0.0).astype(jnp.bfloat16))
-        mass = mass + jnp.where(hit, added[1:2] + added[2:3], 0.0)
-        total = total + added[3:4]
+        masses.append(jnp.where(hit, added[1:2] + added[2:3], 0.0))
+        totals.append(added[3:4])
     choose = jnp.concatenate(chosen, axis=1)[:, : n * stride]
     sums = jnp.dot(choose, values, preferred_element_type=jnp.float32)
-    mass_col = jnp.sum(mass, axis=1, keepdims=True) + 1.0
-    total = jnp.sum(total, axis=1, keepdims=True)
+    mass_col = jnp.sum(tree(masses), axis=1, keepdims=True) + 1.0
+    total = jnp.sum(tree(totals), axis=1, keepdims=True)
     mean_ref[...] = sums * (1.0 / mass_col)
     mass_row = jnp.sum(jnp.where(r_sub == r_lane, mass_col, 0.0), axis=0, keepdims=True)
     rarity_ref[...] = (jnp.log(total / (BINS_DEV * n)) - jnp.log(mass_row))[:, :BINS_DEV]
@@ -163,9 +171,10 @@
             pltpu.SemaphoreType.DMA,
             pltpu.SemaphoreType.REGULAR,
             pltpu.VMEM((goals, width), jnp.bfloat16),
+            pltpu.VMEM((2, goals), jnp.float32),
+            pltpu.SemaphoreType.DMA,
             pltpu.VMEM((1, goals), jnp.int32),
             pltpu.VMEM((1, goals), jnp.float32),
-            pltpu.SemaphoreType.DMA((3,)),
         ],
         compiler_params=pltpu.CompilerParams(collective_id=0, has_side_effects=True),
     )(goal_embed, goal_bins.reshape(1, goals), goal_weights.reshape(1, goals))

time: 11.2 us -> 11.1 us (level)
  no operation moved by 1% of the time
where the time goes in v2:
time: 11.1 us; the launch traced here: 11 us
  Pallas kernels  10.3 us (93%)
  between operations  0.64 us (6%)
    pallas_call x1, Pallas kernels, shards(): pl.pallas_call(functools.partial(kernel, across, along, stride), out_shap...  9.68 us
    pallas_call x1, Pallas kernels, shards(): pl.pallas_call(put, out_shape=(jax.ShapeDtypeStruct((BINS_DEV, width), jn...  0.64 us

profile of v2, /device:TPU:0, one launch (start us, length us, event | category | flops | bytes accessed | tf_op | source)
XLA Modules:
  0.0 11.0 jit_solution(11427544158304496949)
XLA Ops:
  0.6 9.7 %shard_map.50 = (f32[64,128]{1,0:T(8,128)S(1)}, f32[1,64]{1,0:T(1,128)S(1)}) custom-call(bf16[128,128]{1,0:T(8,128)(2,1)} %embed_hbm.1, s32[1,128]{1,0:T(1,128)} %bitcast.3, f32[1,128]{1,0:T(1,128)} %bitcast.4), custom_call_target="tpu_custom_call" | custom-call | tf_op jit(solution)/shard_map/pallas_call | solution.py:159
  10.3 0.6 %shard_map.51 = (f32[64,128]{1,0:T(8,128)}, f32[1,64]{1,0:T(1,128)}) custom-call(f32[64,128]{1,0:T(8,128)S(1)} %get-tuple-element.6.mean, f32[1,64]{1,0:T(1,128)S(1)} %get-tuple-element.7.rarity), custom_call_target="tpu_custom_call" | custom-call | tf_op jit(solution)/shard_map/pallas_call | solution.py:181

commit v3 on v2

--- a/solution.py
+++ b/solution.py
@@ -10,6 +10,7 @@
 BINS_DEV = 64
 MARKS = 4
 LATE = 6
+LEAD = 8
 LOGICAL = pl.DeviceIdType.LOGICAL
 
 
@@ -39,12 +40,14 @@
 
 
 def kernel(across, along, stride, embed_hbm, bins_hbm, weights_hbm, mean_ref, rarity_ref, send, recv, send_sem, recv_sem, gate, embed_ref, pair_ref, in_sem, bins_ref, weights_ref):
+    n = across * along
+    goals, width = embed_ref.shape
+    for i in range(1):
+        part = pl.ds(i * (goals // 1), goals // 1)
+        pltpu.make_async_copy(embed_hbm.at[part], embed_ref.at[part], send_sem).start()
     pltpu.make_async_copy(bins_hbm, bins_ref, in_sem).start()
     pltpu.make_async_copy(weights_hbm, weights_ref, in_sem).start()
     embed_load = pltpu.make_async_copy(embed_hbm, embed_ref, send_sem)
-    embed_load.start()
-    n = across * along
-    goals, width = embed_ref.shape
     sent_rows = stride + MARKS
     me = lax.axis_index("gx") * along + lax.axis_index("gy")
     late = min(LATE, n // 2)
@@ -60,41 +63,48 @@
     shift = BINS_DEV.bit_length() - 1
     sub = lax.broadcasted_iota(jnp.int32, (goals, goals), 0)
     lane = lax.broadcasted_iota(jnp.int32, (goals, goals), 1)
-    rows_iota = lax.broadcasted_iota(jnp.int32, (n * stride, goals), 0)
     t_sub = lax.broadcasted_iota(jnp.int32, (stride, goals), 0)
     t_lane = lax.broadcasted_iota(jnp.int32, (stride, goals), 1)
-    before = (sub < lane).astype(jnp.bfloat16)
+    exact = jnp.bfloat16 if n <= 256 else jnp.float32
+    before = (sub < lane).astype(exact)
     pltpu.make_async_copy(pair_ref, pair_ref, in_sem).wait()
     bins = bins_ref[...]
     weights = weights_ref[...]
     owners = lax.shift_right_logical(bins, shift)
     labels = (bins - owners * BINS_DEV).astype(jnp.float32)
     hi, lo = split2(weights)
-    owners_row = jnp.broadcast_to(owners.astype(jnp.float32), (goals, goals)).astype(jnp.bfloat16)
-    same = jnp.where(owners_row.T == owners_row, before, jnp.bfloat16(0))
+    owners_row = jnp.broadcast_to(owners.astype(jnp.float32), (goals, goals)).astype(exact)
+    same = jnp.where(owners_row.T == owners_row, before, exact(0))
     same = tree([same[i : i + 16] for i in range(0, goals, 16)])
     place = jnp.sum(same.astype(jnp.float32), axis=0, keepdims=True).astype(jnp.int32)
     weights_col = jnp.broadcast_to(weights, (goals, goals)).T
     embed_load.wait()
     base = lax.rem(me, goals // stride) * stride
     spot = (sub == place + base).astype(jnp.bfloat16)
+    slot = owners * stride + place
     kind = lax.rem(t_sub, MARKS)
     kinds = jnp.where(kind == 0, labels, jnp.where(kind == 1, hi, jnp.where(kind == 2, lo, 0.0)))
-    half = n // 2
-    owner_of = jnp.where(t_sub < MARKS, 0, half)
-    tagged = jnp.concatenate([jnp.where(owner_of + o == owners, kinds, 0.0) for o in range(half)], axis=0).astype(jnp.bfloat16)
-    marks = lax.dot_general(tagged, spot, (((1,), (1,)), ((), ())), preferred_element_type=jnp.float32)
-    marks = marks.reshape(half, stride, goals)
-    marks = jnp.concatenate([marks, jnp.roll(marks, -MARKS, axis=1)], axis=0)
     scaled = (weights_col[:, :width] * embed_ref[...].astype(jnp.float32)).astype(jnp.bfloat16)
-    pick = (rows_iota == owners * stride + place).astype(jnp.bfloat16)
-    rows = jnp.dot(pick, scaled, preferred_element_type=jnp.float32)
     local = jnp.sum(weights, axis=1, keepdims=True)
     total = jnp.zeros((stride, goals), jnp.float32)
     for i, part in enumerate(split3(local)):
         total = jnp.where((t_sub == 3) & (t_lane == i), part, total)
-    marks = marks + total[None]
-    send[...] = jnp.concatenate([rows.reshape(n, stride, width), marks], axis=1).astype(jnp.bfloat16)
+
+    def pack(first, count):
+        half = count // 2
+        rows_iota = lax.broadcasted_iota(jnp.int32, (count * stride, goals), 0) + first * stride
+        rows = jnp.dot((rows_iota == slot).astype(jnp.bfloat16), scaled, preferred_element_type=jnp.float32)
+        owner_of = jnp.where(t_sub < MARKS, first, first + half)
+        tagged = [jnp.where(owner_of + o == owners, kinds, 0.0) for o in range(half)]
+        tagged = jnp.concatenate(tagged, axis=0).astype(jnp.bfloat16)
+        marks = lax.dot_general(tagged, spot, (((1,), (1,)), ((), ())), preferred_element_type=jnp.float32)
+        marks = marks.reshape(half, stride, goals)
+        marks = jnp.concatenate([marks, jnp.roll(marks, -MARKS, axis=1)], axis=0) + total[None]
+        both = jnp.concatenate([rows.reshape(count, stride, width), marks], axis=1)
+        send[first : first + count] = both.astype(jnp.bfloat16)
+
+    lead = min(LEAD, early)
+    pack(0, lead)
 
     def start(d):
         pltpu.make_async_remote_copy(
@@ -107,12 +117,16 @@
         ).start()
 
     pl.semaphore_wait(barrier, jnp.where(is_late, early, early - 1))
-    each(0, early, lambda d: pl.when(me != d)(lambda: start(d)))
+    each(0, lead, lambda d: pl.when(me != d)(lambda: start(d)))
     pl.when(is_late)(lambda: each(0, early, lambda d: signal(gate, d)))
+    pack(lead, n - lead)
+    each(lead, early, lambda d: pl.when(me != d)(lambda: start(d)))
     pl.semaphore_wait(gate, jnp.where(is_late, 1, late))
     each(early, n, lambda d: pl.when(me == d - late)(lambda: signal(gate, d)))
     each(early, n, lambda d: pl.when(me != d)(lambda: start(d)))
     recv[me] = send[me]
+    sent = send.at[pl.ds(0, n - 1), pl.ds(0, sent_rows)]
+    pltpu.make_async_copy(sent, sent, send_sem).wait()
     landed = recv.at[pl.ds(0, n - 1), pl.ds(0, sent_rows)]
     pltpu.make_async_copy(landed, landed, recv_sem).wait()
 
@@ -137,8 +151,6 @@
     mean_ref[...] = sums * (1.0 / mass_col)
     mass_row = jnp.sum(jnp.where(r_sub == r_lane, mass_col, 0.0), axis=0, keepdims=True)
     rarity_ref[...] = (jnp.log(total / (BINS_DEV * n)) - jnp.log(mass_row))[:, :BINS_DEV]
-    sent = send.at[pl.ds(0, n - 1), pl.ds(0, sent_rows)]
-    pltpu.make_async_copy(sent, sent, send_sem).wait()
 
 
 def put(mean, rarity, mean_hbm, rarity_hbm, sem):

time: 11.1 us -> 11.1 us (level)
  no operation moved by 1% of the time
where the time goes in v3:
time: 11.1 us; the launch traced here: 10.9 us
  Pallas kernels  10.3 us (93%)
  between operations  0.64 us (6%)
    pallas_call x1, Pallas kernels, shards(): pl.pallas_call(functools.partial(kernel, across, along, stride), out_shap...  9.67 us
    pallas_call x1, Pallas kernels, shards(): pl.pallas_call(put, out_shape=(jax.ShapeDtypeStruct((BINS_DEV, width), jn...  0.64 us

profile of v3, /device:TPU:0, one launch (start us, length us, event | category | flops | bytes accessed | tf_op | source)
XLA Modules:
  0.0 10.9 jit_solution(3363193971870076912)
XLA Ops:
  0.6 9.7 %shard_map.50 = (f32[64,128]{1,0:T(8,128)S(1)}, f32[1,64]{1,0:T(1,128)S(1)}) custom-call(bf16[128,128]{1,0:T(8,128)(2,1)} %embed_hbm.1, s32[1,128]{1,0:T(1,128)} %bitcast.3, f32[1,128]{1,0:T(1,128)} %bitcast.4), custom_call_target="tpu_custom_call" | custom-call | tf_op jit(solution)/shard_map/pallas_call | solution.py:171
  10.3 0.6 %shard_map.51 = (f32[64,128]{1,0:T(8,128)}, f32[1,64]{1,0:T(1,128)}) custom-call(f32[64,128]{1,0:T(8,128)S(1)} %get-tuple-element.6.mean, f32[1,64]{1,0:T(1,128)S(1)} %get-tuple-element.7.rarity), custom_call_target="tpu_custom_call" | custom-call | tf_op jit(solution)/shard_map/pallas_call | solution.py:193

commit v4 on v3

--- a/solution.py
+++ b/solution.py
@@ -42,12 +42,10 @@
 def kernel(across, along, stride, embed_hbm, bins_hbm, weights_hbm, mean_ref, rarity_ref, send, recv, send_sem, recv_sem, gate, embed_ref, pair_ref, in_sem, bins_ref, weights_ref):
     n = across * along
     goals, width = embed_ref.shape
-    for i in range(1):
-        part = pl.ds(i * (goals // 1), goals // 1)
-        pltpu.make_async_copy(embed_hbm.at[part], embed_ref.at[part], send_sem).start()
+    embed_load = pltpu.make_async_copy(embed_hbm, embed_ref, send_sem)
+    embed_load.start()
     pltpu.make_async_copy(bins_hbm, bins_ref, in_sem).start()
     pltpu.make_async_copy(weights_hbm, weights_ref, in_sem).start()
-    embed_load = pltpu.make_async_copy(embed_hbm, embed_ref, send_sem)
     sent_rows = stride + MARKS
     me = lax.axis_index("gx") * along + lax.axis_index("gy")
     late = min(LATE, n // 2)
@@ -125,8 +123,6 @@
     each(early, n, lambda d: pl.when(me == d - late)(lambda: signal(gate, d)))
     each(early, n, lambda d: pl.when(me != d)(lambda: start(d)))
     recv[me] = send[me]
-    sent = send.at[pl.ds(0, n - 1), pl.ds(0, sent_rows)]
-    pltpu.make_async_copy(sent, sent, send_sem).wait()
     landed = recv.at[pl.ds(0, n - 1), pl.ds(0, sent_rows)]
     pltpu.make_async_copy(landed, landed, recv_sem).wait()
 
@@ -151,6 +147,8 @@
     mean_ref[...] = sums * (1.0 / mass_col)
     mass_row = jnp.sum(jnp.where(r_sub == r_lane, mass_col, 0.0), axis=0, keepdims=True)
     rarity_ref[...] = (jnp.log(total / (BINS_DEV * n)) - jnp.log(mass_row))[:, :BINS_DEV]
+    sent = send.at[pl.ds(0, n - 1), pl.ds(0, sent_rows)]
+    pltpu.make_async_copy(sent, sent, send_sem).wait()
 
 
 def put(mean, rarity, mean_hbm, rarity_hbm, sem):

time: 11.1 us -> 11.1 us (level)
  no operation moved by 1% of the time
where the time goes in v4:
time: 11.1 us; the launch traced here: 10.9 us
  Pallas kernels  10.3 us (93%)
  between operations  0.64 us (6%)
    pallas_call x1, Pallas kernels, shards(): pl.pallas_call(functools.partial(kernel, across, along, stride), out_shap...  9.67 us
    pallas_call x1, Pallas kernels, shards(): pl.pallas_call(put, out_shape=(jax.ShapeDtypeStruct((BINS_DEV, width), jn...  0.64 us

profile of v4, /device:TPU:0, one launch (start us, length us, event | category | flops | bytes accessed | tf_op | source)
XLA Modules:
  0.0 10.9 jit_solution(5331634050725986693)
XLA Ops:
  0.6 9.7 %shard_map.50 = (f32[64,128]{1,0:T(8,128)S(1)}, f32[1,64]{1,0:T(1,128)S(1)}) custom-call(bf16[128,128]{1,0:T(8,128)(2,1)} %embed_hbm.1, s32[1,128]{1,0:T(1,128)} %bitcast.3, f32[1,128]{1,0:T(1,128)} %bitcast.4), custom_call_target="tpu_custom_call" | custom-call | tf_op jit(solution)/shard_map/pallas_call | solution.py:169
  10.3 0.6 %shard_map.51 = (f32[64,128]{1,0:T(8,128)}, f32[1,64]{1,0:T(1,128)}) custom-call(f32[64,128]{1,0:T(8,128)S(1)} %get-tuple-element.6.mean, f32[1,64]{1,0:T(1,128)S(1)} %get-tuple-element.7.rarity), custom_call_target="tpu_custom_call" | custom-call | tf_op jit(solution)/shard_map/pallas_call | solution.py:191

commit v5 on v3

--- a/solution.py
+++ b/solution.py
@@ -117,8 +117,8 @@
         ).start()
 
     pl.semaphore_wait(barrier, jnp.where(is_late, early, early - 1))
+    pl.when(is_late)(lambda: each(0, early, lambda d: signal(gate, d)))
     each(0, lead, lambda d: pl.when(me != d)(lambda: start(d)))
-    pl.when(is_late)(lambda: each(0, early, lambda d: signal(gate, d)))
     pack(lead, n - lead)
     each(lead, early, lambda d: pl.when(me != d)(lambda: start(d)))
     pl.semaphore_wait(gate, jnp.where(is_late, 1, late))

time: 11.1 us -> 11.1 us (level)
  no operation moved by 1% of the time
where the time goes in v5:
time: 11.1 us; the launch traced here: 11 us
  Pallas kernels  10.3 us (93%)
  between operations  0.64 us (6%)
    pallas_call x1, Pallas kernels, shards(): pl.pallas_call(functools.partial(kernel, across, along, stride), out_shap...  9.68 us
    pallas_call x1, Pallas kernels, shards(): pl.pallas_call(put, out_shape=(jax.ShapeDtypeStruct((BINS_DEV, width), jn...  0.64 us

profile of v5, /device:TPU:0, one launch (start us, length us, event | category | flops | bytes accessed | tf_op | source)
XLA Modules:
  0.0 11.0 jit_solution(10260996476678310598)
XLA Ops:
  0.6 9.7 %shard_map.50 = (f32[64,128]{1,0:T(8,128)S(1)}, f32[1,64]{1,0:T(1,128)S(1)}) custom-call(bf16[128,128]{1,0:T(8,128)(2,1)} %embed_hbm.1, s32[1,128]{1,0:T(1,128)} %bitcast.3, f32[1,128]{1,0:T(1,128)} %bitcast.4), custom_call_target="tpu_custom_call" | custom-call | tf_op jit(solution)/shard_map/pallas_call | solution.py:171
  10.3 0.6 %shard_map.51 = (f32[64,128]{1,0:T(8,128)}, f32[1,64]{1,0:T(1,128)}) custom-call(f32[64,128]{1,0:T(8,128)S(1)} %get-tuple-element.6.mean, f32[1,64]{1,0:T(1,128)S(1)} %get-tuple-element.7.rarity), custom_call_target="tpu_custom_call" | custom-call | tf_op jit(solution)/shard_map/pallas_call | solution.py:193

commit v6 on v3

--- a/solution.py
+++ b/solution.py
@@ -10,7 +10,7 @@
 BINS_DEV = 64
 MARKS = 4
 LATE = 6
-LEAD = 8
+LEAD = 16
 LOGICAL = pl.DeviceIdType.LOGICAL
 
 

time: 11.1 us -> 11.1 us (level)
  no operation moved by 1% of the time
where the time goes in v6:
time: 11.1 us; the launch traced here: 10.9 us
  Pallas kernels  10.3 us (93%)
  between operations  0.64 us (6%)
    pallas_call x1, Pallas kernels, shards(): pl.pallas_call(functools.partial(kernel, across, along, stride), out_shap...  9.67 us
    pallas_call x1, Pallas kernels, shards(): pl.pallas_call(put, out_shape=(jax.ShapeDtypeStruct((BINS_DEV, width), jn...  0.64 us

profile of v6, /device:TPU:0, one launch (start us, length us, event | category | flops | bytes accessed | tf_op | source)
XLA Modules:
  0.0 10.9 jit_solution(18118348221023906509)
XLA Ops:
  0.6 9.7 %shard_map.50 = (f32[64,128]{1,0:T(8,128)S(1)}, f32[1,64]{1,0:T(1,128)S(1)}) custom-call(bf16[128,128]{1,0:T(8,128)(2,1)} %embed_hbm.1, s32[1,128]{1,0:T(1,128)} %bitcast.3, f32[1,128]{1,0:T(1,128)} %bitcast.4), custom_call_target="tpu_custom_call" | custom-call | tf_op jit(solution)/shard_map/pallas_call | solution.py:171
  10.3 0.6 %shard_map.51 = (f32[64,128]{1,0:T(8,128)}, f32[1,64]{1,0:T(1,128)}) custom-call(f32[64,128]{1,0:T(8,128)S(1)} %get-tuple-element.6.mean, f32[1,64]{1,0:T(1,128)S(1)} %get-tuple-element.7.rarity), custom_call_target="tpu_custom_call" | custom-call | tf_op jit(solution)/shard_map/pallas_call | solution.py:193
